TPU v7x, 32 devices: a whole 2x2x4 slice. The times are simulated.
32 devices in a mesh: col: 16 (over z, y, x), row: 2 (over core).
Axes of the slice: x: 2, y: 2, z: 4, core: 2. Of those that a mesh axis runs over, the one named last changes fastest.
Arguments:
- kernel: float32 [512, 131072], P('row', 'col'), may hold values from -0.0234375 to 0.0234375
- slip_deficit: float32 [64, 131072], P(None, ('col', 'row')), may hold values from -6 to 6
- loading: float32 [512], P('row'), may hold values from -4 to 4
- direct_effect: float32 [512], P('row'), may hold values from 1 to 4
- log_state: float32 [64, 512], P(None, 'row'), may hold values from -1 to 1
Outputs:
- slip_rate: float32 [64, 512], P(None, 'row')
- next_state: float32 [64, 512], P(None, 'row')
All inputs are finite; a program needn't handle non-finite values. Where the computation divides by a largest or mean magnitude, that divisor is 1e-20 or more.
Results may differ from a plain program's by a relative error of at most 0.00013.
Values sent between devices are 32-bit elements; how exact they have to be, the bound alone decides.
A program may use at most 64 MiB of HBM per device.

v0:
```python
import jax
import jax.numpy as jnp
from jax import lax
from jax.sharding import PartitionSpec as P


def friction(stress, direct_effect, log_state):
    return 2.0 * jnp.exp(-log_state) * jnp.sinh(stress / direct_effect[None, :])


def evolve(log_state, slip_rate, peak_rate):
    step_size = 1.0 / (peak_rate + 1e-06)
    return log_state + step_size[:, None] * (jnp.exp(-log_state) - jnp.abs(slip_rate))


def on_device(kernel, slip_deficit, loading, direct_effect, log_state):
    partial_stress = lax.dot_general(
        lax.all_gather(slip_deficit, "row", axis=1, tiled=True),
        kernel,
        (((1,), (1,)), ((), ())),
        precision=lax.Precision.HIGHEST,
        preferred_element_type=jnp.float32,
    )
    stress = lax.psum(partial_stress, "col") + loading[None, :]
    slip_rate = friction(stress, direct_effect, log_state)
    peak_rate = lax.pmax(jnp.max(jnp.abs(slip_rate), axis=1), "row")
    next_state = evolve(log_state, slip_rate, peak_rate)
    return (slip_rate, next_state)


def solution(mesh):
    return jax.shard_map(
        on_device,
        mesh=mesh,
        in_specs=(P("row", "col"), P(None, ("col", "row")), P("row"), P("row"), P(None, "row")),
        out_specs=(P(None, "row"), P(None, "row")),
        check_vma=False,
    )
```

profile of v0, /device:TPU:0, one launch (start us, length us, event | category | flops | bytes accessed | tf_op | source)
XLA Modules:
  0.0 151.2 jit_solution(1238443934083582144)
XLA Ops:
  7.2 0.0 copy-start
  7.2 0.0 copy-start.2
  7.2 0.0 copy-start.3
  7.2 0.0 all-gather.2.cloned.1.call-start
  7.2 0.7 all-gather.2.cloned.1.call-update
  7.9 0.0 all-reduce.2.cloned.1.call-start
  8.0 14.9 %all-gather.2.cloned.1.call-done = f32[64,8192]{1,0:T(8,128)} async-done(((f32[64,4096]{1,0:T(8,128)}), f32[64,8192]{1,0:T(8,128)}) %all-gather.2.cloned.1.call-update) | async-done | bytes 2097168 | tf_op jit(solution)/shard_map/all_gather | solution.py:18
  22.9 12.4 %fusion.4 = f32[64,256]{1,0:T(8,128)} fusion(f32[64,8192]{1,0:T(8,128)} %all-gather.2.cloned.1.call-done, f32[256,8192]{1,0:T(8,128)} %param.5), kind=kOutput, calls=%fused_computation.9 | convolution fusion | flops 1610612736 | bytes 10551296 | tf_op jit(solution)/shard_map/dot_general | solution.py:17
  35.3 0.0 all-reduce.2.cloned.1.call-update
  35.3 104.8 %all-reduce.2.cloned.1.call-done = f32[64,256]{1,0:T(8,128)} async-done(((f32[64,256]{1,0:T(8,128)}), f32[64,256]{1,0:T(8,128)}) %all-reduce.2.cloned.1.call-update) | async-done | bytes 65552 | tf_op jit(solution)/shard_map/psum | solution.py:24
  140.1 0.0 copy-done
  140.1 0.0 copy-done.2
  140.1 0.0 copy-done.3
  140.1 1.0 abs_reduce_fusion
  141.1 0.0 copy-start.1
  141.1 2.5 %pmax.7 = f32[64]{0:T(128)S(1)} all-reduce(f32[64]{0:T(128)S(1)} %get-tuple-element.2), channel_id=1, replica_groups=mesh['col'=16,'row'=2] {'row'}, use_global_device_ids=true, to_apply=%region_2.0 | all-reduce | flops 64 | bytes 512 | tf_op jit(solution)/shard_map/pmax | solution.py:26
  143.6 0.7 multiply_add_fusion
  144.3 0.0 copy-done.1
  (1 shorter events, 0.0 us)
Async XLA Ops:
  7.2 132.9 %copy-start = (f32[64,256]{1,0:T(8,128)S(1)}, f32[64,256]{1,0:T(8,128)}, u32[]{:S(2)}) copy-start(f32[64,256]{1,0:T(8,128)} %param.9) | copy-start | bytes 196612
  7.2 132.9 %copy-start.2 = (f32[256]{0:T(256)S(1)}, f32[256]{0:T(256)}, u32[]{:S(2)}) copy-start(f32[256]{0:T(256)} %param.8) | copy-start | bytes 3076
  7.2 132.9 %copy-start.3 = (f32[256]{0:T(256)S(1)}, f32[256]{0:T(256)}, u32[]{:S(2)}) copy-start(f32[256]{0:T(256)} %param.7) | copy-start | bytes 3076
  7.2 15.7 %all-gather.2.cloned.1.call-start = ((), (), s32[]{:S(2)}) async-start(), calls=%async_computation | async-start | bytes 3145728 | tf_op jit(solution)/shard_map/all_gather | solution.py:18
  7.9 132.2 %all-reduce.2.cloned.1.call-start = ((), (), s32[]{:S(2)}) async-start(), calls=%async_computation.1 | async-start | bytes 131072 | tf_op jit(solution)/shard_map/psum | solution.py:24
  141.1 3.2 %copy-start.1 = (f32[64,256]{1,0:T(8,128)}, f32[64,256]{1,0:T(8,128)S(1)}, u32[]{:S(2)}) copy-start(f32[64,256]{1,0:T(8,128)S(1)} %get-tuple-element.3) | copy-start | bytes 196612
Sparse Core Ops, SparseCore 0:
  9.5 13.2 all-gather.1
  35.4 104.6 all-reduce.1
where the time goes:
time: 151 us
  waiting for transfers between devices  120 us (79%)
  between operations  14.1 us (9%)
  matrix products  12.4 us (8%)
  blocking collectives  2.47 us (2%)
  other arithmetic  1.74 us (1%)
    psum x1, waiting for transfers between devices, on_device(): stress = lax.psum(partial_stress, 'col') + loading[None, :]  105 us
    all_gather x1, waiting for transfers between devices, on_device(): lax.all_gather(slip_deficit, 'row', axis=1, tiled=True)  14.9 us
    dot_general x1, matrix products, on_device(): lax.dot_general(lax.all_gather(slip_deficit, 'row', axis=1, tiled=True),...  12.4 us
  transfers between devices with their start and end apart: 2, of which 2 were waited for; matrix products, arithmetic and copies ran while one was open for 0% of the time, Pallas kernels for 0%

commit v1 on v0

v1 whole, which is shorter than its diff:
```python
import functools
import math

import jax
import jax.numpy as jnp
from jax import lax
from jax.experimental import pallas as pl
from jax.experimental.pallas import tpu as pltpu
from jax.sharding import PartitionSpec as P

MESH = pl.DeviceIdType.MESH
LANES = 128
LOG_HALF = math.log(0.5)


def sinh(x):
    square = x * x
    series = 1.0 / 362880.0
    for order in (5040.0, 120.0, 6.0, 1.0):
        series = series * square + 1.0 / order
    wide = jnp.exp(x + LOG_HALF) - jnp.exp(LOG_HALF - x)
    return jnp.where(jnp.abs(x) < 1.0, x * series, wide)


def split(x):
    high = x.astype(jnp.bfloat16)
    return high, (x - high.astype(jnp.float32)).astype(jnp.bfloat16)


def times_transposed(a, b):
    return lax.dot_general(a, b, (((1,), (1,)), ((), ())), preferred_element_type=jnp.float32)


def body(
    cols, rows, owners, chunk,
    kernel_hbm, slip_hbm, loading_hbm, effect_hbm, state_hbm,
    rate_ref, next_ref,
    kernel_buf, slip_buf, total, loading_all, effect_all, state_all,
    state_box, out_box, in_box, peak_out, peak_in, step_all,
    kernel_sem, slip_sem, swap_send, swap_recv, aux_sem, aux_send, aux_recv,
    sum_send, sum_recv, gather_send, gather_recv,
):
    n = cols * rows
    col, row = lax.axis_index("col"), lax.axis_index("row")
    me = col * rows + row
    members, width = state_hbm.shape
    share = members // owners
    half = slip_hbm.shape[1]
    pieces = half // chunk

    def place(target):
        return {"col": lax.div(target, rows), "row": lax.rem(target, rows)}

    barrier = pltpu.get_barrier_semaphore()

    def greet(k, carry):
        pl.semaphore_signal(barrier, inc=1, device_id=place(lax.rem(me + k, n)), device_id_type=MESH)
        return carry

    lax.fori_loop(1, n, greet, 0)

    for j in range(pieces):
        pltpu.make_async_copy(slip_hbm.at[:, pl.ds(j * chunk, chunk)], slip_buf.at[j], slip_sem.at[j]).start()
    extras = ((loading_hbm, loading_all), (effect_hbm, effect_all), (state_hbm, state_all))
    for i, (src, dst) in enumerate(extras):
        pltpu.make_async_copy(src, dst.at[0], aux_sem.at[i]).start()
    for h in range(rows):
        base = lax.rem(row + h, rows) * half
        for j in range(pieces):
            start = pl.multiple_of(base + j * chunk, chunk)
            pltpu.make_async_copy(kernel_hbm.at[:, pl.ds(start, chunk)], kernel_buf.at[h * pieces + j], kernel_sem.at[h * pieces + j]).start()

    def multiply(j):
        pltpu.make_async_copy(kernel_hbm.at[:, pl.ds(0, chunk)], kernel_buf.at[j], kernel_sem.at[j]).wait()
        slip_high, slip_low = split(slip_buf[j])
        kernel_high, kernel_low = split(kernel_buf[j])
        both = times_transposed(jnp.concatenate([slip_high, slip_low], axis=0), kernel_high)
        return both[:members] + both[members:] + times_transposed(slip_high, kernel_low)

    total[...] = jnp.zeros_like(total)

    def own(j, carry):
        pltpu.make_async_copy(slip_hbm.at[:, pl.ds(0, chunk)], slip_buf.at[j], slip_sem.at[j]).wait()
        total[...] += multiply(j)
        return carry

    lax.fori_loop(0, pieces, own, 0)

    for i, (src, dst) in enumerate(extras):
        pltpu.make_async_copy(src, dst.at[0], aux_sem.at[i]).wait()
    pl.semaphore_wait(barrier, n - 1)

    def swap(h, j):
        other = lax.rem(row + rows - h, rows)
        return pltpu.make_async_remote_copy(
            src_ref=slip_buf.at[j], dst_ref=slip_buf.at[h * pieces + j],
            send_sem=swap_send.at[h * pieces + j], recv_sem=swap_recv.at[h * pieces + j],
            device_id={"col": col, "row": other}, device_id_type=MESH)

    def aux(h):
        other = lax.rem(row + rows - h, rows)
        return [
            pltpu.make_async_remote_copy(
                src_ref=dst.at[0], dst_ref=dst.at[h], send_sem=aux_send.at[h, i], recv_sem=aux_recv.at[h, i],
                device_id={"col": col, "row": other}, device_id_type=MESH)
            for i, (src, dst) in enumerate(extras)
        ]

    for h in range(1, rows):
        for j in range(pieces):
            swap(h, j).start()
        for copy in aux(h):
            copy.start()

    for h in range(1, rows):
        def others(j, carry):
            swap(h, j).wait_recv()
            total[...] += multiply(h * pieces + j)
            return carry

        lax.fori_loop(0, pieces, others, 0)

    value = total[...]
    for o in range(owners):
        out_box[o] = value[o * share:(o + 1) * share]

    def send_sum(target):
        return pltpu.make_async_remote_copy(
            src_ref=out_box.at[target], dst_ref=in_box.at[me], send_sem=sum_send, recv_sem=sum_recv,
            device_id=place(target), device_id_type=MESH)

    def send_rate(target):
        return pltpu.make_async_remote_copy(
            src_ref=peak_out.at[lax.rem(target, rows)], dst_ref=peak_in.at[me], send_sem=gather_send, recv_sem=gather_recv,
            device_id=place(target), device_id_type=MESH)

    def when_owner(device, act):
        if owners == n:
            act()
        else:
            pl.when(device < owners)(act)

    def spread(k, carry):
        target = lax.rem(me + k, n)
        when_owner(target, lambda: send_sum(target).start())
        return carry

    lax.fori_loop(1, n, spread, 0)

    for h in range(1, rows):
        for copy in aux(h):
            copy.wait_recv()
    for h in range(rows):
        for o in range(owners):
            state_box[h, o] = state_all[h, o * share:(o + 1) * share]

    def finish_member_share():
        in_box[me] = out_box[me]
        blocks = in_box.at[pl.ds(0, n - 1)]
        pltpu.make_async_copy(blocks, blocks, sum_recv).wait()
        rates = []
        for q in range(rows):
            h = lax.rem(q - row + rows, rows)
            parts = [in_box[c * rows + q] for c in range(cols)]
            while len(parts) > 1:
                parts = [parts[i] + parts[i + 1] if i + 1 < len(parts) else parts[i] for i in range(0, len(parts), 2)]
            stress = parts[0] + loading_all[h]
            rates.append(2.0 * jnp.exp(-state_box[h, me]) * sinh(stress / effect_all[h]))
        peak = functools.reduce(jnp.maximum, [jnp.max(jnp.abs(rate), axis=1, keepdims=True) for rate in rates])
        step = jnp.broadcast_to(1.0 / (peak + 1e-6), (share, LANES))
        for q in range(rows):
            peak_out[q, :, :width] = rates[q]
            peak_out[q, :, width:] = step
        peak_in[me] = peak_out[row]

        def share_out(k, carry):
            send_rate(lax.rem(me + k, n)).start()
            return carry

        lax.fori_loop(1, n, share_out, 0)

    when_owner(me, finish_member_share)

    decay = jnp.exp(-state_all[0])

    def await_all(sem, box, sent):
        for count, condition in sent:
            def act():
                blocks = box.at[pl.ds(0, count)]
                pltpu.make_async_copy(blocks, blocks, sem).wait()
            if condition is None:
                act()
            else:
                pl.when(condition)(act)

    if owners == n:
        mine_or_not = [(n - 1, None)]
    else:
        mine_or_not = [(owners - 1, me < owners), (owners, me >= owners)]
    await_all(gather_recv, peak_in, mine_or_not)

    for o in range(owners):
        block = peak_in[o]
        rate_ref[o * share:(o + 1) * share, :] = block[:, :width]
        step_all[o * share:(o + 1) * share, :] = block[:, width:]
    rate = rate_ref[...]
    step = step_all[...]
    for w in range(0, width, LANES):
        lanes = slice(w, w + LANES)
        next_ref[:, lanes] = state_all[0, :, lanes] + step * (decay[:, lanes] - jnp.abs(rate[:, lanes]))

    await_all(sum_send, out_box, mine_or_not)
    if owners == n:
        await_all(gather_send, peak_in, [(n - 1, None)])
    else:
        def sent_all():
            def once(k, carry):
                send_rate(lax.rem(me + k, n)).wait_send()
                return carry
            lax.fori_loop(1, n, once, 0)
        pl.when(me < owners)(sent_all)
    for h in range(1, rows):
        for j in range(pieces):
            swap(h, j).wait_send()
        for copy in aux(h):
            copy.wait_send()


def solution(mesh):
    cols, rows = mesh.shape["col"], mesh.shape["row"]
    n = cols * rows

    def on_device(kernel, slip_deficit, loading, direct_effect, log_state):
        members, width = log_state.shape
        half = slip_deficit.shape[1]
        owners = max(d for d in range(1, min(n, members) + 1) if members % d == 0)
        share = members // owners
        chunk = math.gcd(half, 1024)
        pieces = half // chunk
        slots = rows * pieces
        f32 = jnp.float32
        vmem = pl.BlockSpec(memory_space=pltpu.VMEM)
        hbm = pl.BlockSpec(memory_space=pl.ANY)
        return pl.pallas_call(
            functools.partial(body, cols, rows, owners, chunk),
            out_shape=[jax.ShapeDtypeStruct((members, width), f32)] * 2,
            in_specs=[hbm] * 5,
            out_specs=[vmem, vmem],
            scratch_shapes=[
                pltpu.VMEM((slots, width, chunk), f32),
                pltpu.VMEM((slots, members, chunk), f32),
                pltpu.VMEM((members, width), f32),
                pltpu.VMEM((rows, 1, width), f32),
                pltpu.VMEM((rows, 1, width), f32),
                pltpu.VMEM((rows, members, width), f32),
                pltpu.VMEM((rows, owners, share, width), f32),
                pltpu.VMEM((owners, share, width), f32),
                pltpu.VMEM((n, share, width), f32),
                pltpu.VMEM((rows, share, width + LANES), f32),
                pltpu.VMEM((owners, share, width + LANES), f32),
                pltpu.VMEM((members, LANES), f32),
                pltpu.SemaphoreType.DMA((slots,)),
                pltpu.SemaphoreType.DMA((pieces,)),
                pltpu.SemaphoreType.DMA((slots,)),
                pltpu.SemaphoreType.DMA((slots,)),
                pltpu.SemaphoreType.DMA((3,)),
                pltpu.SemaphoreType.DMA((rows, 3)),
                pltpu.SemaphoreType.DMA((rows, 3)),
                pltpu.SemaphoreType.DMA,
                pltpu.SemaphoreType.DMA,
                pltpu.SemaphoreType.DMA,
                pltpu.SemaphoreType.DMA,
            ],
            compiler_params=pltpu.CompilerParams(
                collective_id=0, has_side_effects=True, vmem_limit_bytes=63 * 2**20
            ),
        )(kernel, slip_deficit, loading.reshape(1, -1), direct_effect.reshape(1, -1), log_state)

    return jax.shard_map(
        on_device,
        mesh=mesh,
        in_specs=(P("row", "col"), P(None, ("col", "row")), P("row"), P("row"), P(None, "row")),
        out_specs=(P(None, "row"), P(None, "row")),
        check_vma=False,
    )
```

time: 151 us -> 24.6 us (0.16)
  waiting for transfers between devices: 120 us -> 0 us
  Pallas kernels: 0 us -> 20.8 us
  between operations: 14.1 us -> 0.64 us
  matrix products: 12.4 us -> 0 us
  local copies, waits for them, and re-layouts: 0.02 us -> 2.95 us
  blocking collectives: 2.47 us -> 0 us
  other arithmetic: 1.74 us -> 0 us
    psum x1 -> x0, waiting for transfers between devices: 105 us -> none  [on_device(): stress = lax.psum(partial_stress, 'col') + loading[None, :]]
    pallas_call x0 -> x1, Pallas kernels: none -> 20.8 us  [on_device(): pl.pallas_call(functools.partial(body, cols, rows, owners, chunk), out_sh...]
    all_gather x1 -> x0, waiting for transfers between devices: 14.9 us -> none  [on_device(): lax.all_gather(slip_deficit, 'row', axis=1, tiled=True)]
    dot_general x1 -> x0, matrix products: 12.4 us -> none  [on_device(): lax.dot_general(lax.all_gather(slip_deficit, 'row', axis=1, tiled=True),...]
    unnamed x8 -> x2, local copies, waits for them, and re-layouts: 0.02 us -> 2.95 us
    pmax x1 -> x0, blocking collectives: 2.47 us -> none  [on_device(): peak_rate = lax.pmax(jnp.max(jnp.abs(slip_rate), axis=1), 'row')]
  transfers between devices with their start and end apart: 2 -> 0, of which waited for: 2 -> 0; matrix products, arithmetic and copies ran while one was open for 0% -> 0% of each run, Pallas kernels for 0% -> 0%
where the time goes in v1:
time: 24.6 us; the launch traced here: 24.4 us
  Pallas kernels  20.8 us (85%)
  local copies, waits for them, and re-layouts  2.95 us (12%)
  between operations  0.64 us (3%)
    pallas_call x1, Pallas kernels, on_device(): pl.pallas_call(functools.partial(body, cols, rows, owners, chunk), out_sh...  20.8 us
    unnamed x2, local copies, waits for them, and re-layouts  2.95 us

profile of v1, /device:TPU:0, one launch (start us, length us, event | category | flops | bytes accessed | tf_op | source)
XLA Modules:
  0.0 24.4 jit_solution(10640800977451066549)
XLA Ops:
  0.6 20.8 %shard_map.68 = (f32[64,256]{1,0:T(8,128)}, f32[64,256]{1,0:T(8,128)}) custom-call(f32[256,8192]{1,0:T(8,128)} %kernel_hbm.1, f32[64,4096]{1,0:T(8,128)} %slip_hbm.1, f32[1,256]{1,0:T(1,128)} %bitcast.2, f32[1,256]{1,0:T(1,128)} %bitcast.3, f32[64,256]{1,0:T(8,128)} %state_hbm.1), custom_call_target="tpu_custom_call" | custom-call | tf_op jit(solution)/shard_map/pallas_call | solution.py:244
  21.5 1.5 %copy.9 = f32[64,256]{1,0:T(8,128)} copy(f32[64,256]{1,0:T(8,128)} %get-tuple-element.4) | data formatting | bytes 131072
  22.9 1.5 %copy.10 = f32[64,256]{1,0:T(8,128)} copy(f32[64,256]{1,0:T(8,128)} %get-tuple-element.5) | data formatting | bytes 131072

commit v2 on v1

--- a/solution.py
+++ b/solution.py
@@ -38,7 +38,7 @@
     kernel_buf, slip_buf, total, loading_all, effect_all, state_all,
     state_box, out_box, in_box, peak_out, peak_in, step_all,
     kernel_sem, slip_sem, swap_send, swap_recv, aux_sem, aux_send, aux_recv,
-    sum_send, sum_recv, gather_send, gather_recv,
+    sum_send, sum_recv, gather_send, gather_recv, hello, ready,
 ):
     n = cols * rows
     col, row = lax.axis_index("col"), lax.axis_index("row")
@@ -52,12 +52,11 @@
         return {"col": lax.div(target, rows), "row": lax.rem(target, rows)}
 
     barrier = pltpu.get_barrier_semaphore()
-
-    def greet(k, carry):
-        pl.semaphore_signal(barrier, inc=1, device_id=place(lax.rem(me + k, n)), device_id_type=MESH)
-        return carry
-
-    lax.fori_loop(1, n, greet, 0)
+    leads = row == 1
+
+    @pl.when(leads)
+    def _():
+        pl.semaphore_signal(barrier, inc=1, device_id={"col": col, "row": 0}, device_id_type=MESH)
 
     for j in range(pieces):
         pltpu.make_async_copy(slip_hbm.at[:, pl.ds(j * chunk, chunk)], slip_buf.at[j], slip_sem.at[j]).start()
@@ -70,26 +69,6 @@
             start = pl.multiple_of(base + j * chunk, chunk)
             pltpu.make_async_copy(kernel_hbm.at[:, pl.ds(start, chunk)], kernel_buf.at[h * pieces + j], kernel_sem.at[h * pieces + j]).start()
 
-    def multiply(j):
-        pltpu.make_async_copy(kernel_hbm.at[:, pl.ds(0, chunk)], kernel_buf.at[j], kernel_sem.at[j]).wait()
-        slip_high, slip_low = split(slip_buf[j])
-        kernel_high, kernel_low = split(kernel_buf[j])
-        both = times_transposed(jnp.concatenate([slip_high, slip_low], axis=0), kernel_high)
-        return both[:members] + both[members:] + times_transposed(slip_high, kernel_low)
-
-    total[...] = jnp.zeros_like(total)
-
-    def own(j, carry):
-        pltpu.make_async_copy(slip_hbm.at[:, pl.ds(0, chunk)], slip_buf.at[j], slip_sem.at[j]).wait()
-        total[...] += multiply(j)
-        return carry
-
-    lax.fori_loop(0, pieces, own, 0)
-
-    for i, (src, dst) in enumerate(extras):
-        pltpu.make_async_copy(src, dst.at[0], aux_sem.at[i]).wait()
-    pl.semaphore_wait(barrier, n - 1)
-
     def swap(h, j):
         other = lax.rem(row + rows - h, rows)
         return pltpu.make_async_remote_copy(
@@ -106,11 +85,46 @@
             for i, (src, dst) in enumerate(extras)
         ]
 
+    @pl.when(leads)
+    def _():
+        pl.semaphore_wait(hello, 1)
+
+        def greet(k, carry):
+            pl.semaphore_signal(barrier, inc=1, device_id={"col": lax.rem(col + k, cols), "row": 1}, device_id_type=MESH)
+            return carry
+
+        lax.fori_loop(1, cols, greet, 0)
+
+    @pl.when(jnp.logical_not(leads))
+    def _():
+        pl.semaphore_wait(barrier, 1)
+        pl.semaphore_signal(hello, inc=1, device_id={"col": col, "row": 1}, device_id_type=MESH)
+
+    for j in range(pieces):
+        pltpu.make_async_copy(slip_hbm.at[:, pl.ds(0, chunk)], slip_buf.at[j], slip_sem.at[j]).wait()
+        for h in range(1, rows):
+            swap(h, j).start()
+    for i, (src, dst) in enumerate(extras):
+        pltpu.make_async_copy(src, dst.at[0], aux_sem.at[i]).wait()
     for h in range(1, rows):
-        for j in range(pieces):
-            swap(h, j).start()
         for copy in aux(h):
             copy.start()
+
+    def multiply(j):
+        pltpu.make_async_copy(kernel_hbm.at[:, pl.ds(0, chunk)], kernel_buf.at[j], kernel_sem.at[j]).wait()
+        slip_high, slip_low = split(slip_buf[j])
+        kernel_high, kernel_low = split(kernel_buf[j])
+        both = times_transposed(jnp.concatenate([slip_high, slip_low], axis=0), kernel_high)
+        return both[:members] + both[members:] + times_transposed(slip_high, kernel_low)
+
+    total[...] = jnp.zeros_like(total)
+
+    def own(j, carry):
+        total[...] += multiply(j)
+        return carry
+
+    lax.fori_loop(0, pieces, own, 0)
+
 
     for h in range(1, rows):
         def others(j, carry):
@@ -119,6 +133,15 @@
             return carry
 
         lax.fori_loop(0, pieces, others, 0)
+
+    @pl.when(leads)
+    def _():
+        pl.semaphore_wait(barrier, cols - 1)
+        pl.semaphore_signal(ready, inc=1, device_id={"col": col, "row": 0}, device_id_type=MESH)
+
+    @pl.when(jnp.logical_not(leads))
+    def _():
+        pl.semaphore_wait(ready, 1)
 
     value = total[...]
     for o in range(owners):
@@ -226,6 +249,17 @@
             copy.wait_send()
 
 
+def write_out(rate_vmem, next_vmem, rate_hbm, next_hbm, sem):
+    copies = [
+        pltpu.make_async_copy(src, dst, sem.at[i])
+        for i, (src, dst) in enumerate(((rate_vmem, rate_hbm), (next_vmem, next_hbm)))
+    ]
+    for copy in copies:
+        copy.start()
+    for copy in copies:
+        copy.wait()
+
+
 def solution(mesh):
     cols, rows = mesh.shape["col"], mesh.shape["row"]
     n = cols * rows
@@ -240,10 +274,11 @@
         slots = rows * pieces
         f32 = jnp.float32
         vmem = pl.BlockSpec(memory_space=pltpu.VMEM)
-        hbm = pl.BlockSpec(memory_space=pl.ANY)
-        return pl.pallas_call(
+        hbm = pl.BlockSpec(memory_space=pltpu.HBM)
+        results = [jax.ShapeDtypeStruct((members, width), f32)] * 2
+        held = pl.pallas_call(
             functools.partial(body, cols, rows, owners, chunk),
-            out_shape=[jax.ShapeDtypeStruct((members, width), f32)] * 2,
+            out_shape=[pltpu.VMEM((members, width), f32)] * 2,
             in_specs=[hbm] * 5,
             out_specs=[vmem, vmem],
             scratch_shapes=[
@@ -270,11 +305,21 @@
                 pltpu.SemaphoreType.DMA,
                 pltpu.SemaphoreType.DMA,
                 pltpu.SemaphoreType.DMA,
+                pltpu.SemaphoreType.REGULAR,
+                pltpu.SemaphoreType.REGULAR,
             ],
             compiler_params=pltpu.CompilerParams(
-                collective_id=0, has_side_effects=True, vmem_limit_bytes=63 * 2**20
+                collective_id=0, has_side_effects=True, vmem_limit_bytes=20 * 2**20
             ),
-        )(kernel, slip_deficit, loading.reshape(1, -1), direct_effect.reshape(1, -1), log_state)
+        )(*(pltpu.with_memory_space_constraint(x, pltpu.HBM) for x in (kernel, slip_deficit, loading.reshape(1, -1), direct_effect.reshape(1, -1), log_state)))
+        return pl.pallas_call(
+            write_out,
+            out_shape=results,
+            in_specs=[vmem] * 2,
+            out_specs=[hbm] * 2,
+            scratch_shapes=[pltpu.SemaphoreType.DMA((2,))],
+            compiler_params=pltpu.CompilerParams(vmem_limit_bytes=2**20),
+        )(*held)
 
     return jax.shard_map(
         on_device,

time: 24.6 us -> 20.8 us (0.85)
  local copies, waits for them, and re-layouts: 2.95 us -> 0 us
  Pallas kernels: 20.8 us -> 20 us
    unnamed x2 -> x0, local copies, waits for them, and re-layouts: 2.95 us -> none
    pallas_call x1, Pallas kernels: 20.8 us -> 19.3 us  [on_device(): pl.pallas_call(functools.partial(body, cols, rows, owners, chunk), out_sh...]
    pallas_call x0 -> x1, Pallas kernels: none -> 0.67 us  [on_device(): pl.pallas_call(write_out, out_shape=results, in_specs=[vmem] * 2, out_spe...]
where the time goes in v2:
time: 20.8 us; the launch traced here: 20.6 us
  Pallas kernels  20 us (96%)
  between operations  0.64 us (3%)
    pallas_call x1, Pallas kernels, on_device(): pl.pallas_call(functools.partial(body, cols, rows, owners, chunk), out_sh...  19.3 us
    pallas_call x1, Pallas kernels, on_device(): pl.pallas_call(write_out, out_shape=results, in_specs=[vmem] * 2, out_spe...  0.67 us

profile of v2, /device:TPU:0, one launch (start us, length us, event | category | flops | bytes accessed | tf_op | source)
XLA Modules:
  0.0 20.6 jit_solution(12868435556323139549)
XLA Ops:
  0.6 19.3 %shard_map.68 = (f32[64,256]{1,0:T(8,128)S(1)}, f32[64,256]{1,0:T(8,128)S(1)}) custom-call(f32[256,8192]{1,0:T(8,128)} %kernel_hbm.1, f32[64,4096]{1,0:T(8,128)} %slip_hbm.1, f32[1,256]{1,0:T(1,128)} %bitcast.2, f32[1,256]{1,0:T(1,128)} %bitcast.3, f32[64,256]{1,0:T(8,128)} %state_hbm.1), custom_call_target="tpu_custom_call" | custom-call | tf_op jit(solution)/shard_map/pallas_call | solution.py:279
  20.0 0.7 %shard_map.69 = (f32[64,256]{1,0:T(8,128)}, f32[64,256]{1,0:T(8,128)}) custom-call(f32[64,256]{1,0:T(8,128)S(1)} %get-tuple-element.4.rate_vmem, f32[64,256]{1,0:T(8,128)S(1)} %get-tuple-element.5.next_vmem), custom_call_target="tpu_custom_call" | custom-call | tf_op jit(solution)/shard_map/pallas_call | solution.py:315

commit v3 on v2

--- a/solution.py
+++ b/solution.py
@@ -269,7 +269,7 @@
         half = slip_deficit.shape[1]
         owners = max(d for d in range(1, min(n, members) + 1) if members % d == 0)
         share = members // owners
-        chunk = math.gcd(half, 1024)
+        chunk = math.gcd(half, 2048)
         pieces = half // chunk
         slots = rows * pieces
         f32 = jnp.float32

time: 20.8 us -> 19.8 us (0.952)
  Pallas kernels: 20 us -> 19 us
    pallas_call x1, Pallas kernels: 19.3 us -> 18.3 us  [on_device(): pl.pallas_call(functools.partial(body, cols, rows, owners, chunk), out_sh...]
where the time goes in v3:
time: 19.8 us; the launch traced here: 19.6 us
  Pallas kernels  19 us (96%)
  between operations  0.64 us (3%)
    pallas_call x1, Pallas kernels, on_device(): pl.pallas_call(functools.partial(body, cols, rows, owners, chunk), out_sh...  18.3 us
    pallas_call x1, Pallas kernels, on_device(): pl.pallas_call(write_out, out_shape=results, in_specs=[vmem] * 2, out_spe...  0.67 us

profile of v3, /device:TPU:0, one launch (start us, length us, event | category | flops | bytes accessed | tf_op | source)
XLA Modules:
  0.0 19.6 jit_solution(12231255862593359681)
XLA Ops:
  0.6 18.3 %shard_map.68 = (f32[64,256]{1,0:T(8,128)S(1)}, f32[64,256]{1,0:T(8,128)S(1)}) custom-call(f32[256,8192]{1,0:T(8,128)} %kernel_hbm.1, f32[64,4096]{1,0:T(8,128)} %slip_hbm.1, f32[1,256]{1,0:T(1,128)} %bitcast.2, f32[1,256]{1,0:T(1,128)} %bitcast.3, f32[64,256]{1,0:T(8,128)} %state_hbm.1), custom_call_target="tpu_custom_call" | custom-call | tf_op jit(solution)/shard_map/pallas_call | solution.py:279
  19.0 0.7 %shard_map.69 = (f32[64,256]{1,0:T(8,128)}, f32[64,256]{1,0:T(8,128)}) custom-call(f32[64,256]{1,0:T(8,128)S(1)} %get-tuple-element.4.rate_vmem, f32[64,256]{1,0:T(8,128)S(1)} %get-tuple-element.5.next_vmem), custom_call_target="tpu_custom_call" | custom-call | tf_op jit(solution)/shard_map/pallas_call | solution.py:315
